TPU v7x, 32 devices: a whole 2x2x4 slice. The times are simulated.
32 devices in a mesh: row: 8 (over z, y), col: 4 (over x, core).
Axes of the slice: x: 2, y: 2, z: 4, core: 2. Of those that a mesh axis runs over, the one named last changes fastest.
Arguments:
- x_blocks: bfloat16 [128, 8, 128, 128], P('row', 'col')
- x_cols: int32 [128, 8], P('row', 'col'), may hold values from 0 to 31, as said below
- x_count: int32 [128, 4], P('row', 'col'), may hold values from 0 to 2, as said below
- y_cols: int32 [128, 48], P('row', 'col'), may hold values from 0 to 31, as said below
- y_count: int32 [128, 4], P('row', 'col'), may hold values from 0 to 12, as said below
- branch_flag: int32 [128], P('row'), may hold values from 0 to 1
Outputs:
- new_blocks: bfloat16 [128, 48, 128, 128], P('row', 'col')
- new_trace: float32 [1], replicated
Inputs may be any that keep to these rules, and one draw needn't show every extreme that they name: `x_cols`: within one block row and one column group, the first x_count slots name distinct block columns; other slots hold arbitrary valid columns. Slot 0 of block row I in group I // 32 names column I % 32. `x_count`: reaches 2; at least 1 for block row I in group I // 32. `y_cols`: within one block row and one column group, the first y_count slots name distinct block columns. Slot 0 of block row I in group I // 32 names column I % 32. `y_count`: reaches 12; at least 1 for block row I in group I // 32.
All inputs are finite; a program needn't handle non-finite values.
Results may differ from a plain program's by a relative error of at most 0.0004.
Values may be sent and summed in bfloat16 or wider, within the bound.
No kernel may reach another device: no remote copies, remote signals or barrier semaphores. Data moves between devices by JAX's collectives and lax.ppermute only.
A program may use at most 128 MiB of HBM per device.

v0:
```python
import jax
import jax.numpy as jnp
from jax import lax
from jax.sharding import PartitionSpec as P

NB = 128
ROWCAP = 2


def pick_blocks(blocks, cols, count, block_keys, wanted, active, offset):
    height = cols.shape[0]
    slot_count = cols.shape[1]
    relative = block_keys - offset
    inside = (relative >= 0) & (relative < height) & active
    clipped = jnp.clip(relative, 0, height - 1).astype(jnp.int32)
    slot_ids = jnp.arange(slot_count, dtype=jnp.int32)
    matched = (
        (cols[clipped] == wanted[..., None])
        & (slot_ids < count[clipped, 0][..., None])
        & inside[..., None]
    )
    found = jnp.any(matched, axis=-1)
    picked = jnp.sum(jnp.where(matched, slot_ids, 0), axis=-1)
    flat_blocks = blocks.reshape((height * slot_count,) + blocks.shape[2:])
    chosen = flat_blocks[clipped * slot_count + picked]
    return jnp.where(found[..., None, None], chosen, jnp.zeros((), blocks.dtype))


def pair_keys(row_cols, row_count, y_cols, y_count, col_width, slot_count):
    pairs = row_cols.shape[1]
    ycap = y_cols.shape[1]
    pair_ids = jnp.arange(pairs, dtype=jnp.int32)
    groups = pair_ids // slot_count
    block_keys = groups[None, :] * col_width + row_cols
    live = (pair_ids % slot_count)[None, :] < jnp.take(row_count, groups, axis=1)
    y_live = jnp.arange(ycap, dtype=jnp.int32)[None, :] < y_count
    shape = (row_cols.shape[0], ycap, pairs)
    block_keys = jnp.broadcast_to(block_keys[:, None, :], shape)
    wanted = jnp.broadcast_to(y_cols[:, :, None], shape)
    active = live[:, None, :] & y_live[:, :, None]
    return (block_keys, wanted, active)


def contract(row_blocks, panel, block_keys, wanted, active, offset):

    def one_row(items):
        row_block, keys, targets, flags = items
        chosen = pick_blocks(panel[0], panel[1], panel[2], keys, targets, flags, offset)
        return jnp.einsum("pab,ypbc->yac", row_block, chosen, preferred_element_type=jnp.float32)

    return lax.map(one_row, (row_blocks, block_keys, wanted, active))


def finish(
    product, own_blocks, own_cols, own_count, y_cols, y_count, branch_flag, row_start, col_start
):
    ycap = y_cols.shape[1]
    y_live = jnp.arange(ycap, dtype=jnp.int32)[None, :] < y_count
    slot_ids = jnp.arange(own_cols.shape[1], dtype=jnp.int32)
    own_match = (own_cols[:, None, :] == y_cols[:, :, None]) & (
        slot_ids[None, None, :] < own_count[:, :, None]
    )
    own_term = jnp.einsum(
        "iyq,iqab->iyab", own_match.astype(jnp.float32), own_blocks.astype(jnp.float32)
    )
    flip = (branch_flag == 1)[:, None, None, None]
    updated = jnp.where(flip, 2.0 * own_term - product, product)
    updated = jnp.where(y_live[..., None, None], updated, jnp.zeros((), updated.dtype))
    rows_global = row_start + jnp.arange(y_cols.shape[0], dtype=jnp.int32)[:, None]
    cols_global = col_start + y_cols
    diagonal = (rows_global == cols_global) & y_live
    traces = jnp.trace(updated, axis1=2, axis2=3)
    trace_part = jnp.sum(jnp.where(diagonal, traces, jnp.zeros((), traces.dtype)))
    return (updated.astype(jnp.bfloat16), trace_part)


def on_device(x_blocks, x_cols, x_count, y_cols, y_count, branch_flag):
    row_blocks, row_cols, row_count = (
        lax.all_gather(x_blocks, "col", axis=1, tiled=True),
        lax.all_gather(x_cols, "col", axis=1, tiled=True),
        lax.all_gather(x_count, "col", axis=1, tiled=True),
    )
    col_width = NB // lax.axis_size("col")
    block_keys, wanted, active = pair_keys(row_cols, row_count, y_cols, y_count, col_width, ROWCAP)
    panel = (
        lax.all_gather(x_blocks, "row", axis=0, tiled=True),
        lax.all_gather(x_cols, "row", axis=0, tiled=True),
        lax.all_gather(x_count, "row", axis=0, tiled=True),
    )
    product = contract(row_blocks, panel, block_keys, wanted, active, 0)
    row_start = lax.axis_index("row") * x_blocks.shape[0]
    col_start = lax.axis_index("col") * col_width
    updated, trace_part = finish(
        product, x_blocks, x_cols, x_count, y_cols, y_count, branch_flag, row_start, col_start
    )
    total = lax.psum(trace_part, ("row", "col"))
    return (updated, total.reshape((1,)))


def solution(mesh):
    return jax.shard_map(
        on_device,
        mesh=mesh,
        in_specs=(
            P("row", "col", None, None),
            P("row", "col"),
            P("row", "col"),
            P("row", "col"),
            P("row", "col"),
            P("row"),
        ),
        out_specs=(P("row", "col", None, None), P()),
        check_vma=False,
    )
```

profile of v0, /device:TPU:0, one launch (start us, length us, event | category | flops | bytes accessed | tf_op | source)
XLA Modules:
  0.0 493.7 jit_solution(7032172679561146887)
XLA Ops:
  8.7 6.2 %all-gather.2 = s32[4,1,16]{2,1,0:T(1,128)S(1)} all-gather(s32[1,1,16]{2,1,0:T(1,128)} %bitcast.93), channel_id=1, replica_groups=mesh['row'=8,'col'=4] {'col'}, dimensions={0}, use_global_device_ids=true | all-gather | bytes 320 | tf_op jit(solution)/shard_map/all_gather | solution.py:81
  16.4 5.5 %all-gather = s32[4,2,16]{2,1,0:T(2,128)S(1)} all-gather(s32[1,2,16]{2,1,0:T(2,128)} %bitcast.91), channel_id=1, replica_groups=mesh['row'=8,'col'=4] {'col'}, dimensions={0}, use_global_device_ids=true | all-gather | bytes 640 | tf_op jit(solution)/shard_map/all_gather | solution.py:80
  22.1 21.3 %all-gather.1 = s32[8,16,2]{1,2,0:T(2,128)S(1)} all-gather(s32[1,16,2]{1,2,0:T(2,128)} %bitcast.92), channel_id=1, replica_groups=mesh['row'=8,'col'=4] {'row'}, dimensions={0}, use_global_device_ids=true | all-gather | bytes 1152 | tf_op jit(solution)/shard_map/all_gather | solution.py:87
  46.1 6.8 %all-reduce.1 = s32[128]{0:T(128)S(1)} all-reduce(s32[128]{0:T(128)S(1)} %bitcast_dynamic-update-slice_fusion), channel_id=1, replica_groups=mesh['row'=8,'col'=4] {'row'}, use_global_device_ids=true, to_apply=%add.1 | all-reduce | flops 128 | bytes 1024
  55.2 118.2 %all-gather.6.cloned.1.call-done = bf16[128,2,128,128]{3,2,1,0:T(8,128)(2,1)} async-done(((bf16[16,2,128,128]{3,2,1,0:T(8,128)(2,1)}), bf16[128,2,128,128]{3,2,1,0:T(8,128)(2,1)}) %all-gather.6.cloned.1.call-update) | async-done | bytes 8388624 | tf_op jit(solution)/shard_map/all_gather | solution.py:86
  174.2 233.5 %while.10 = (s32[]{:T(128)}, f32[16,12,128,128]{2,3,1,0:T(8,128)}, s32[16,12,8]{1,2,0:T(8,128)S(1)}, s32[128,2]{1,0:T(8,128)S(1)}, s32[16,12,8]{1,2,0:T(8,128)S(...) while((s32[]{:T(128)}, f32[16,12,128,128]{2,3,1,0:T(8,128)}, ...), condition=%wide.region_3.4_spmd, body=%wide.region_0.3_spmd.sunk | while | flops 404230784 | bytes 16804500 | solution.py:51
  177.6 4.5 gather_fusion.2
  182.2 2.8 copy.78
  184.9 3.8 fusion.36
  192.2 4.5 gather_fusion.2
  196.7 2.8 copy.78
  199.5 3.8 fusion.36
  206.8 4.5 gather_fusion.2
  211.3 2.8 copy.78
  214.1 3.8 fusion.36
  221.4 4.5 gather_fusion.2
  225.9 2.8 copy.78
  228.7 3.8 fusion.36
  235.9 4.5 gather_fusion.2
  240.5 2.8 copy.78
  243.3 3.8 fusion.36
  250.5 4.5 gather_fusion.2
  255.1 2.8 copy.78
  257.8 3.8 fusion.36
  265.1 4.5 gather_fusion.2
  272.4 3.8 fusion.36
  279.7 4.5 gather_fusion.2
  287.0 3.9 fusion.36
  294.3 4.5 gather_fusion.2
  301.6 3.8 fusion.36
  308.9 4.5 gather_fusion.2
  316.2 3.8 fusion.36
  323.4 4.5 gather_fusion.2
  330.7 3.9 fusion.36
  338.1 4.5 gather_fusion.2
  345.4 3.9 fusion.36
  352.7 4.5 gather_fusion.2
  360.0 3.8 fusion.36
  367.3 4.5 gather_fusion.2
  374.6 3.9 fusion.36
  381.9 4.5 gather_fusion.2
  389.2 3.8 fusion.36
  396.5 4.5 gather_fusion.2
  403.8 3.8 fusion.36
  407.6 17.6 %copy.52 = f32[16,12,128,128]{3,1,2,0:T(8,128)} copy(f32[16,12,128,128]{2,3,1,0:T(8,128)} %get-tuple-element.49) | data formatting | bytes 25165824 | tf_op jit(solution)/shard_map/while | solution.py:51
  425.3 14.4 %select_reduce_fusion.1 = (f32[16,12]{1,0:T(8,128)S(1)}, bf16[16,12,128,128]{3,1,2,0:T(8,128)(2,1)}) fusion(pred[128,128]{1,0:T(8,128)(4,1)S(1)} %iota_compare_fusion.1, f32[16,12,128,128]{3,1,2,0:T(8,128)} %copy.52, bf16[16,2,128,128]{3,2,1,0:T(8,128)(2,1)S(1)} %copy-done, pred[16,2]{1,0:T(8,128)(4,1)S(1)} %iota_compare_fusion.2, ...), kind=kOutput, calls=%fused_computation.30 | convolution fusion | flops 34603584 | bytes 19941232 | tf_op jit(solution)/shard_map/iyq,iqab->iyab/dot_general | solution.py:63
  440.4 38.5 %psum.7 = f32[1]{0:T(128)} all-reduce(f32[1]{0:T(128)} %bitcast.30), channel_id=1, replica_groups=mesh['row'=8,'col'=4] {'row','col'}, use_global_device_ids=true, to_apply=%region_6.7 | all-reduce | flops 1 | bytes 8 | tf_op jit(solution)/shard_map/psum | solution.py:96
  478.9 8.0 %copy.54 = bf16[16,12,128,128]{3,2,1,0:T(8,128)(2,1)} copy(bf16[16,12,128,128]{3,1,2,0:T(8,128)(2,1)} %get-tuple-element.106) | data formatting | bytes 12582912
  (366 shorter events, 90.9 us)
Async XLA Ops:
  7.2 48.0 %all-gather.8.cloned.1.call-start = ((), (), s32[]{:S(2)}) async-start(), calls=%async_computation.1 | async-start | bytes 5242880 | tf_op jit(solution)/shard_map/all_gather | solution.py:79
  7.9 165.5 %all-gather.6.cloned.1.call-start = ((), (), s32[]{:S(2)}) async-start(), calls=%async_computation | async-start | bytes 9437184 | tf_op jit(solution)/shard_map/all_gather | solution.py:86
  407.6 17.7 %copy-start = (bf16[16,2,128,128]{3,2,1,0:T(8,128)(2,1)S(1)}, bf16[16,2,128,128]{3,2,1,0:T(8,128)(2,1)}, u32[]{:S(2)}) copy-start(bf16[16,2,128,128]{3,2,1,0:T(8,128)(2,1)} %param.8) | copy-start | bytes 3145732
  407.6 17.7 %copy-start.1 = (s32[16,12]{1,0:T(8,128)S(1)}, s32[16,12]{1,0:T(8,128)}, u32[]{:S(2)}) copy-start(s32[16,12]{1,0:T(8,128)} %param.11) | copy-start | bytes 2308
  425.3 14.4 %copy-start.2 = (s32[16,1]{0,1:T(1,128)S(1)}, s32[16,1]{0,1:T(1,128)}, u32[]{:S(2)}) copy-start(s32[16,1]{0,1:T(1,128)} %param.12) | copy-start | bytes 196
Sparse Core Ops, SparseCore 0:
  9.5 37.1 all-gather.7
  48.9 124.4 all-gather.5
where the time goes:
time: 495 us; the launch traced here: 494 us
  local copies, waits for them, and re-layouts  190 us (38%)
  waiting for transfers between devices  120 us (24%)
  blocking collectives  78.3 us (16%)
  matrix products  75.7 us (15%)
  between operations  14.8 us (3%)
  other arithmetic  14.1 us (3%)
    all_gather x1, waiting for transfers between devices, on_device(): lax.all_gather(x_blocks, 'row', axis=0, tiled=True)  118 us
    gather x32, local copies, waits for them, and re-layouts, pick_blocks(): chosen = flat_blocks[clipped * slot_count + picked]  117 us
    dot_general x16, matrix products, one_row(): jnp.einsum('pab,ypbc->yac', row_block, chosen, preferred_element_type=jnp...  61.3 us
    psum x1, blocking collectives, on_device(): total = lax.psum(trace_part, ('row', 'col'))  38.5 us
    all_gather x1, blocking collectives, on_device(): lax.all_gather(x_cols, 'row', axis=0, tiled=True)  21.3 us
    gather x32, local copies, waits for them, and re-layouts, pick_blocks(): count[clipped, 0][..., None]  21 us
    while x2, local copies, waits for them, and re-layouts, contract(): return lax.map(one_row, (row_blocks, block_keys, wanted, active))  17.8 us
    dot_general x1, matrix products, finish(): jnp.einsum('iyq,iqab->iyab', own_match.astype(jnp.float32), own_blocks.as...  14.4 us
  transfers between devices with their start and end apart: 2, of which 1 were waited for; matrix products, arithmetic and copies ran while one was open for 1% of the time, Pallas kernels for 0%

commit v1 on v0

--- a/solution.py
+++ b/solution.py
@@ -93,7 +93,7 @@
     updated, trace_part = finish(
         product, x_blocks, x_cols, x_count, y_cols, y_count, branch_flag, row_start, col_start
     )
-    total = lax.psum(trace_part, ("row", "col"))
+    total = jnp.sum(lax.all_gather(trace_part, ("row", "col")), axis=0)
     return (updated, total.reshape((1,)))
 
 

time: 495 us -> 496 us (level)
    psum x1 -> x0, blocking collectives: 38.5 us -> none  [on_device(): total = lax.psum(trace_part, ('row', 'col'))]
    unnamed x1 -> x2, blocking collectives: 6.77 us -> 45.1 us
    unnamed x11 -> x13, local copies, waits for them, and re-layouts: 10.7 us -> 11.5 us
where the time goes in v1:
time: 496 us; the launch traced here: 495 us
  local copies, waits for them, and re-layouts  191 us (39%)
  waiting for transfers between devices  120 us (24%)
  blocking collectives  78.1 us (16%)
  matrix products  75.7 us (15%)
  between operations  14.8 us (3%)
  other arithmetic  14.7 us (3%)
    all_gather x1, waiting for transfers between devices, on_device(): lax.all_gather(x_blocks, 'row', axis=0, tiled=True)  118 us
    gather x32, local copies, waits for them, and re-layouts, pick_blocks(): chosen = flat_blocks[clipped * slot_count + picked]  117 us
    dot_general x16, matrix products, one_row(): jnp.einsum('pab,ypbc->yac', row_block, chosen, preferred_element_type=jnp...  61.3 us
    unnamed x2, blocking collectives  45.1 us
    all_gather x1, blocking collectives, on_device(): lax.all_gather(x_cols, 'row', axis=0, tiled=True)  21.3 us
    gather x32, local copies, waits for them, and re-layouts, pick_blocks(): count[clipped, 0][..., None]  21 us
    while x2, local copies, waits for them, and re-layouts, contract(): return lax.map(one_row, (row_blocks, block_keys, wanted, active))  17.8 us
    dot_general x1, matrix products, finish(): jnp.einsum('iyq,iqab->iyab', own_match.astype(jnp.float32), own_blocks.as...  14.4 us
  transfers between devices with their start and end apart: 2, of which 1 were waited for; matrix products, arithmetic and copies ran while one was open for 1% of the time, Pallas kernels for 0%

profile of v1, /device:TPU:0, one launch (start us, length us, event | category | flops | bytes accessed | tf_op | source)
XLA Modules:
  0.0 494.8 jit_solution(599962559359370882)
XLA Ops:
  8.7 6.2 %all-gather.2 = s32[4,1,16]{2,1,0:T(1,128)S(1)} all-gather(s32[1,1,16]{2,1,0:T(1,128)} %bitcast.94), channel_id=1, replica_groups=mesh['row'=8,'col'=4] {'col'}, dimensions={0}, use_global_device_ids=true | all-gather | bytes 320 | tf_op jit(solution)/shard_map/all_gather | solution.py:81
  16.4 5.5 %all-gather = s32[4,2,16]{2,1,0:T(2,128)S(1)} all-gather(s32[1,2,16]{2,1,0:T(2,128)} %bitcast.92), channel_id=1, replica_groups=mesh['row'=8,'col'=4] {'col'}, dimensions={0}, use_global_device_ids=true | all-gather | bytes 640 | tf_op jit(solution)/shard_map/all_gather | solution.py:80
  22.1 21.3 %all-gather.1 = s32[8,16,2]{1,2,0:T(2,128)S(1)} all-gather(s32[1,16,2]{1,2,0:T(2,128)} %bitcast.93), channel_id=1, replica_groups=mesh['row'=8,'col'=4] {'row'}, dimensions={0}, use_global_device_ids=true | all-gather | bytes 1152 | tf_op jit(solution)/shard_map/all_gather | solution.py:87
  46.1 6.8 %all-reduce.1 = s32[128]{0:T(128)S(1)} all-reduce(s32[128]{0:T(128)S(1)} %bitcast_dynamic-update-slice_fusion), channel_id=1, replica_groups=mesh['row'=8,'col'=4] {'row'}, use_global_device_ids=true, to_apply=%add.1 | all-reduce | flops 128 | bytes 1024
  55.2 118.2 %all-gather.6.cloned.1.call-done = bf16[128,2,128,128]{3,2,1,0:T(8,128)(2,1)} async-done(((bf16[16,2,128,128]{3,2,1,0:T(8,128)(2,1)}), bf16[128,2,128,128]{3,2,1,0:T(8,128)(2,1)}) %all-gather.6.cloned.1.call-update) | async-done | bytes 8388624 | tf_op jit(solution)/shard_map/all_gather | solution.py:86
  174.2 233.5 %while.10 = (s32[]{:T(128)}, f32[16,12,128,128]{2,3,1,0:T(8,128)}, s32[16,12,8]{1,2,0:T(8,128)S(1)}, s32[128,2]{1,0:T(8,128)S(1)}, s32[16,12,8]{1,2,0:T(8,128)S(...) while((s32[]{:T(128)}, f32[16,12,128,128]{2,3,1,0:T(8,128)}, ...), condition=%wide.region_3.4_spmd, body=%wide.region_0.3_spmd.sunk | while | flops 404230784 | bytes 16804500 | solution.py:51
  177.6 4.5 gather_fusion.2
  182.2 2.8 copy.79
  184.9 3.8 fusion.36
  192.2 4.5 gather_fusion.2
  196.7 2.8 copy.79
  199.5 3.8 fusion.36
  206.8 4.5 gather_fusion.2
  211.3 2.8 copy.79
  214.1 3.8 fusion.36
  221.4 4.5 gather_fusion.2
  225.9 2.8 copy.79
  228.7 3.8 fusion.36
  235.9 4.5 gather_fusion.2
  240.5 2.8 copy.79
  243.3 3.8 fusion.36
  250.5 4.5 gather_fusion.2
  255.1 2.8 copy.79
  257.8 3.8 fusion.36
  265.1 4.5 gather_fusion.2
  272.4 3.8 fusion.36
  279.7 4.5 gather_fusion.2
  287.0 3.9 fusion.36
  294.3 4.5 gather_fusion.2
  301.6 3.8 fusion.36
  308.9 4.5 gather_fusion.2
  316.2 3.8 fusion.36
  323.4 4.5 gather_fusion.2
  330.7 3.9 fusion.36
  338.1 4.5 gather_fusion.2
  345.4 3.9 fusion.36
  352.7 4.5 gather_fusion.2
  360.0 3.8 fusion.36
  367.3 4.5 gather_fusion.2
  374.6 3.9 fusion.36
  381.9 4.5 gather_fusion.2
  389.2 3.8 fusion.36
  396.5 4.5 gather_fusion.2
  403.8 3.8 fusion.36
  407.6 17.6 %copy.52 = f32[16,12,128,128]{3,1,2,0:T(8,128)} copy(f32[16,12,128,128]{2,3,1,0:T(8,128)} %get-tuple-element.49) | data formatting | bytes 25165824 | tf_op jit(solution)/shard_map/while | solution.py:51
  425.3 14.4 %select_reduce_fusion.1 = (f32[16,12]{1,0:T(8,128)S(1)}, bf16[16,12,128,128]{3,1,2,0:T(8,128)(2,1)}) fusion(pred[128,128]{1,0:T(8,128)(4,1)S(1)} %iota_compare_fusion.1, f32[16,12,128,128]{3,1,2,0:T(8,128)} %copy.52, bf16[16,2,128,128]{3,2,1,0:T(8,128)(2,1)S(1)} %copy-done, pred[16,2]{1,0:T(8,128)(4,1)S(1)} %iota_compare_fusion.2, ...), kind=kOutput, calls=%fused_computation.30 | convolution fusion | flops 34603584 | bytes 19941232 | tf_op jit(solution)/shard_map/iyq,iqab->iyab/dot_general | solution.py:63
  441.1 38.3 %all-reduce.2 = f32[32]{0:T(128)S(1)} all-reduce(f32[32]{0:T(128)S(1)} %dynamic-update-slice.1), channel_id=1, replica_groups=mesh['row'=8,'col'=4] {'row','col'}, use_global_device_ids=true, to_apply=%add.2 | all-reduce | flops 32 | bytes 256
  480.0 8.0 %copy.54 = bf16[16,12,128,128]{3,2,1,0:T(8,128)(2,1)} copy(bf16[16,12,128,128]{3,1,2,0:T(8,128)(2,1)} %get-tuple-element.106) | data formatting | bytes 12582912
  (369 shorter events, 92.3 us)
Async XLA Ops:
  7.2 48.0 %all-gather.8.cloned.1.call-start = ((), (), s32[]{:S(2)}) async-start(), calls=%async_computation.1 | async-start | bytes 5242880 | tf_op jit(solution)/shard_map/all_gather | solution.py:79
  7.9 165.5 %all-gather.6.cloned.1.call-start = ((), (), s32[]{:S(2)}) async-start(), calls=%async_computation | async-start | bytes 9437184 | tf_op jit(solution)/shard_map/all_gather | solution.py:86
  407.6 17.7 %copy-start = (bf16[16,2,128,128]{3,2,1,0:T(8,128)(2,1)S(1)}, bf16[16,2,128,128]{3,2,1,0:T(8,128)(2,1)}, u32[]{:S(2)}) copy-start(bf16[16,2,128,128]{3,2,1,0:T(8,128)(2,1)} %param.8) | copy-start | bytes 3145732
  407.6 17.7 %copy-start.1 = (s32[16,12]{1,0:T(8,128)S(1)}, s32[16,12]{1,0:T(8,128)}, u32[]{:S(2)}) copy-start(s32[16,12]{1,0:T(8,128)} %param.11) | copy-start | bytes 2308
  425.3 14.4 %copy-start.2 = (s32[16,1]{0,1:T(1,128)S(1)}, s32[16,1]{0,1:T(1,128)}, u32[]{:S(2)}) copy-start(s32[16,1]{0,1:T(1,128)} %param.12) | copy-start | bytes 196
Sparse Core Ops, SparseCore 0:
  9.5 37.1 all-gather.7
  48.9 124.4 all-gather.5
